TPU v7x, 256 devices: a whole 4x4x8 slice. The times are simulated.
256 devices in a mesh: shard: 64 (over z, x, core), model: 4 (over y).
Axes of the slice: x: 4, y: 4, z: 8, core: 2. Of those that a mesh axis runs over, the one named last changes fastest.
Arguments:
- grad_stack: float32 [512, 128, 2048], P(None, 'shard', 'model'), may hold values from -6 to 6
- moment_stack: float32 [512, 128, 2048], P(None, 'shard', 'model'), may hold values from -6 to 6
- weight_stack: float32 [512, 128, 2048], P(None, 'shard', 'model'), may hold values from -0.1875 to 0.1875
Outputs:
- new_weights: float32 [512, 128, 2048], P(None, 'shard', 'model')
- new_momentum: float32 [512, 128, 2048], P(None, 'shard', 'model')
All inputs are finite; a program needn't handle non-finite values.
Results may differ from a plain program's by a relative error of at most 0.00021.
Values sent between devices are 32-bit elements; how exact they have to be, the bound alone decides.
A program may use at most 64 MiB of HBM per device.

v0:
```python
import jax
import jax.numpy as jnp
from jax import lax
from jax.sharding import PartitionSpec as P

ITERS = 5


hold_rate = 0.95
learn_rate = 1.0
decay_rate = 0.1


def on_device(grad_stack, moment_stack, weight_stack):
    new_momentum = hold_rate * moment_stack + grad_stack
    moved = lax.all_to_all(new_momentum, "shard", split_axis=0, concat_axis=1, tiled=True)
    whole = lax.all_to_all(moved, "model", split_axis=0, concat_axis=2, tiled=True)
    iterate = whole * lax.rsqrt(jnp.sum(whole * whole, axis=(1, 2), keepdims=True) + 1e-06)
    for step in range(ITERS):
        gram = jnp.einsum("mik,mjk->mij", iterate, iterate, precision=lax.Precision.HIGHEST)
        mixed = -4.775 * gram + 2.0315 * jnp.einsum(
            "mij,mjk->mik", gram, gram, precision=lax.Precision.HIGHEST
        )
        iterate = 3.4445 * iterate + jnp.einsum(
            "mij,mjk->mik", mixed, iterate, precision=lax.Precision.HIGHEST
        )
    iterate = lax.all_to_all(iterate, "model", split_axis=2, concat_axis=0, tiled=True)
    back = lax.all_to_all(iterate, "shard", split_axis=1, concat_axis=0, tiled=True)
    new_weights = (1.0 - learn_rate * decay_rate) * weight_stack - learn_rate * back
    return (new_weights, new_momentum)


def solution(mesh):
    in_specs = (P(None, "shard", "model"), P(None, "shard", "model"), P(None, "shard", "model"))
    out_specs = (P(None, "shard", "model"), P(None, "shard", "model"))
    return jax.shard_map(
        on_device, mesh=mesh, in_specs=in_specs, out_specs=out_specs, check_vma=False
    )
```

profile of v0, /device:TPU:1, one launch (start us, length us, event | category | flops | bytes accessed | tf_op | source)
XLA Modules:
  0.0 219.6 jit_solution(1098745697749330971)
XLA Ops:
  0.6 3.7 %multiply_add_fusion = f32[512,2,512]{2,1,0:T(2,128)S(1)} fusion(f32[512,2,512]{2,1,0:T(2,128)} %param.3, f32[512,2,512]{2,1,0:T(2,128)} %param.4), kind=kLoop, calls=%fused_computation.9 | loop fusion | flops 1048576 | bytes 6291456 | tf_op jit(solution)/shard_map/add | solution.py:15
  4.3 62.5 %all_to_all.72 = f32[512,2,512]{2,1,0:T(2,128)S(1)} all-to-all(f32[512,2,512]{2,1,0:T(2,128)S(1)} %multiply_add_fusion), channel_id=1, replica_groups=mesh['shard'=64,'model'=4] {'shard'}, dimensions={0} | all-to-all | bytes 4194304 | tf_op jit(solution)/shard_map/all_to_all | solution.py:16
  66.8 0.4 copy.46
  67.5 1.2 copy.32
  68.7 28.0 %all_to_all.73 = f32[8,128,512]{2,1,0:T(8,128)S(1)} all-to-all(f32[8,128,512]{2,1,0:T(8,128)S(1)} %copy.32), channel_id=1, replica_groups=mesh['shard'=64,'model'=4] {'model'}, dimensions={0} | all-to-all | bytes 4194304 | tf_op jit(solution)/shard_map/all_to_all | solution.py:17
  96.7 0.4 multiply_reduce_fusion
  97.3 2.3 %fusion = f32[2,128,128]{2,1,0:T(8,128)S(1)} fusion(f32[2,128,2048]{2,1,0:T(8,128)S(1)} %bitcast.47, f32[2]{0:T(128)S(1)} %add_rsqrt_fusion), kind=kOutput, calls=%fused_computation.10 | convolution fusion | flops 805830656 | bytes 2228232 | tf_op jit(solution)/shard_map/mik,mjk->mij/dot_general | solution.py:20
  99.9 2.1 convolution_add_fusion.4
  102.0 2.0 fusion.10
  104.4 2.1 convolution_add_fusion.3
  106.5 2.0 fusion.11
  108.5 0.3 fusion.5
  108.8 2.3 %convolution_add_fusion.2 = f32[2,128,2048]{2,1,0:T(8,128)S(1)} fusion(f32[2,128,128]{2,1,0:T(8,128)S(1)} %fusion.5, f32[2,128,2048]{2,1,0:T(8,128)S(1)} %convolution_add_fusion.3), kind=kOutput, calls=%fused_computation.2 | convolution fusion | flops 806354944 | bytes 4325376 | tf_op jit(solution)/shard_map/mij,mjk->mik/dot_general | solution.py:24
  111.1 2.0 fusion.12
  113.4 2.1 convolution_add_fusion.1
  115.5 2.0 fusion.13
  117.8 2.1 convolution_add_fusion
  119.9 2.3 %copy.34 = f32[2,128,2048]{1,0,2:T(2,128)} copy(f32[2,128,2048]{2,1,0:T(8,128)S(1)} %convolution_add_fusion) | data formatting | bytes 4194304 | tf_op jit(solution)/shard_map/add | solution.py:24
  122.3 26.8 %all_to_all.74 = f32[2,128,2048]{1,0,2:T(2,128)S(1)} all-to-all(f32[2,128,2048]{1,0,2:T(2,128)} %copy.34), channel_id=1, replica_groups=mesh['shard'=64,'model'=4] {'model'}, dimensions={2} | all-to-all | bytes 4194304 | tf_op jit(solution)/shard_map/all_to_all | solution.py:27
  149.2 1.8 copy.36
  151.0 2.8 %copy.37 = f32[8,128,512]{2,0,1:T(8,128)S(1)} copy(f32[8,128,512]{2,1,0:T(8,128)} %bitcast.55) | data formatting | bytes 4194304 | tf_op jit(solution)/shard_map/all_to_all | solution.py:27
  153.8 62.2 %all_to_all.75 = f32[8,128,512]{2,0,1:T(8,128)S(1)} all-to-all(f32[8,128,512]{2,0,1:T(8,128)S(1)} %copy.37), channel_id=1, replica_groups=mesh['shard'=64,'model'=4] {'shard'}, dimensions={1} | all-to-all | bytes 4194304 | tf_op jit(solution)/shard_map/all_to_all | solution.py:28
  216.0 0.6 bitcast_subtract_fusion
  216.6 2.9 %copy.39 = f32[512,2,512]{2,1,0:T(2,128)} copy(f32[512,2,512]{2,0,1:T(8,128)S(1)} %bitcast_subtract_fusion) | data formatting | bytes 4194304
  (12 shorter events, 1.7 us)
Async XLA Ops:
  4.3 62.9 %copy-start = (f32[512,2,512]{2,1,0:T(2,128)}, f32[512,2,512]{2,1,0:T(2,128)S(1)}, u32[]{:S(2)}) copy-start(f32[512,2,512]{2,1,0:T(2,128)S(1)} %multiply_add_fusion) | copy-start | bytes 6291460
  153.8 62.2 %copy-start.1 = (f32[512,2,512]{2,1,0:T(2,128)S(1)}, f32[512,2,512]{2,1,0:T(2,128)}, u32[]{:S(2)}) copy-start(f32[512,2,512]{2,1,0:T(2,128)} %param.5) | copy-start | bytes 6291460
where the time goes:
time: 220 us
  blocking collectives  180 us (82%)
  matrix products  22.5 us (10%)
  local copies, waits for them, and re-layouts  12.1 us (6%)
  other arithmetic  4.62 us (2%)
    all_to_all x1, blocking collectives, on_device(): lax.all_to_all(new_momentum, 'shard', split_axis=0, concat_axis=1, tiled=...  62.5 us
    all_to_all x1, blocking collectives, on_device(): lax.all_to_all(iterate, 'shard', split_axis=1, concat_axis=0, tiled=True)  62.2 us
    all_to_all x1, blocking collectives, on_device(): lax.all_to_all(moved, 'model', split_axis=0, concat_axis=2, tiled=True)  28 us
    all_to_all x1, blocking collectives, on_device(): lax.all_to_all(iterate, 'model', split_axis=2, concat_axis=0, tiled=True)  26.8 us
    dot_general x5, matrix products, on_device(): jnp.einsum('mij,mjk->mik', mixed, iterate, precision=lax.Precision.HIGHEST)  10.7 us
    dot_general x5, matrix products, on_device(): jnp.einsum('mik,mjk->mij', iterate, iterate, precision=lax.Precision.HIGH...  10.4 us
    all_to_all x3, local copies, waits for them, and re-layouts, on_device(): lax.all_to_all(iterate, 'model', split_axis=2, concat_axis=0, tiled=True)  4.76 us

commit v1 on v0

v1 whole, which is shorter than its diff:
```python
import jax
import jax.numpy as jnp
from jax import lax
from jax.sharding import PartitionSpec as P

hold_rate = 0.95
learn_rate = 1.0
decay_rate = 0.1
HIGH = lax.Precision.HIGHEST


def mul(a, b):
    return jnp.einsum("mij,mjk->mik", a, b, precision=HIGH)


def chain(gram, steps):
    eye = jnp.eye(gram.shape[-1], dtype=gram.dtype)
    total = None
    for step in range(steps):
        factor = 3.4445 * eye - 4.775 * gram + 2.0315 * mul(gram, gram)
        total = factor if total is None else mul(factor, total)
        if step < steps - 1:
            gram = mul(mul(factor, gram), factor)
    return total


def summed_gram(rows):
    part = jnp.einsum("mik,mjk->mij", rows, rows, precision=HIGH)
    parts = lax.all_to_all(part, "model", split_axis=0, concat_axis=0, tiled=True)
    return parts.reshape(4, -1, *parts.shape[1:]).sum(axis=0)


def on_device(grad_stack, moment_stack, weight_stack):
    new_momentum = hold_rate * moment_stack + grad_stack
    rows = lax.all_to_all(new_momentum, "shard", split_axis=0, concat_axis=1, tiled=True)
    gram = summed_gram(rows)
    scale = lax.rsqrt(jnp.trace(gram, axis1=1, axis2=2)[:, None, None] + 1e-06)
    first = chain(gram * scale * scale, 2) * scale
    rows = mul(lax.all_gather(first, "model", axis=0, tiled=True), rows)
    second = chain(summed_gram(rows), 3)
    rows = mul(lax.all_gather(second, "model", axis=0, tiled=True), rows)
    back = lax.all_to_all(rows, "shard", split_axis=1, concat_axis=0, tiled=True)
    new_weights = (1.0 - learn_rate * decay_rate) * weight_stack - learn_rate * back
    return (new_weights, new_momentum)


def solution(mesh):
    spec = P(None, "shard", "model")
    return jax.shard_map(on_device, mesh=mesh, in_specs=(spec,) * 3, out_specs=(spec,) * 2, check_vma=False)
```

time: 220 us -> 199 us (0.905)
  blocking collectives: 180 us -> 158 us
  matrix products: 22.5 us -> 12.5 us
  waiting for transfers between devices: 0 us -> 6.93 us
  starting transfers between devices: 0 us -> 4.18 us
  local copies, waits for them, and re-layouts: 12.1 us -> 7.95 us
  other arithmetic: 4.62 us -> 7.12 us
    all_to_all x3 -> x2, blocking collectives: 117 us -> 75.6 us  [the longest x1 66.2 us: on_device(): lax.all_to_all(rows, 'shard', split_axis=1, concat_axis=0, tiled=True)]
    all_gather x0 -> x2, blocking collectives: none -> 20.4 us  [the longest x1 10.5 us: on_device(): rows = mul(lax.all_gather(second, 'model', axis=0, tiled=True), rows)]
    dot_general x15 -> x18, matrix products: 22.5 us -> 12.5 us  [the longest x16 7.59 us: mul(): return jnp.einsum('mij,mjk->mik', a, b, precision=HIGH)]
    all_to_all x0 -> x1, waiting for transfers between devices: none -> 6.93 us  [summed_gram(): lax.all_to_all(part, 'model', split_axis=0, concat_axis=0, tiled=True)]
    all_to_all x0 -> x1, starting transfers between devices: none -> 4.18 us  [summed_gram(): lax.all_to_all(part, 'model', split_axis=0, concat_axis=0, tiled=True)]
    all_to_all x4 -> x1, local copies, waits for them, and re-layouts: 5 us -> 1.93 us  [on_device(): lax.all_to_all(rows, 'shard', split_axis=1, concat_axis=0, tiled=True)]
    unnamed x5 -> x8, local copies, waits for them, and re-layouts: 2.95 us -> 0.02 us
    all_to_all x3 -> x2, local copies, waits for them, and re-layouts: 1.86 us -> 4.78 us  [on_device(): lax.all_to_all(new_momentum, 'shard', split_axis=0, concat_axis=1, tiled=...]
  transfers between devices with their start and end apart: 0 -> 1, of which waited for: 0 -> 1; matrix products, arithmetic and copies ran while one was open for 0% -> 0% of each run, Pallas kernels for 0% -> 0%
where the time goes in v1:
time: 199 us; the launch traced here: 198 us
  blocking collectives  158 us (79%)
  matrix products  12.5 us (6%)
  local copies, waits for them, and re-layouts  7.95 us (4%)
  other arithmetic  7.12 us (4%)
  waiting for transfers between devices  6.93 us (3%)
  starting transfers between devices  4.18 us (2%)
    all_to_all x1, blocking collectives, on_device(): lax.all_to_all(rows, 'shard', split_axis=1, concat_axis=0, tiled=True)  66.2 us
    all_to_all x1, blocking collectives, on_device(): lax.all_to_all(new_momentum, 'shard', split_axis=0, concat_axis=1, tiled=...  62.5 us
    all_gather x1, blocking collectives, on_device(): rows = mul(lax.all_gather(second, 'model', axis=0, tiled=True), rows)  10.5 us
    all_gather x1, blocking collectives, on_device(): rows = mul(lax.all_gather(first, 'model', axis=0, tiled=True), rows)  9.9 us
    all_to_all x1, blocking collectives, summed_gram(): lax.all_to_all(part, 'model', split_axis=0, concat_axis=0, tiled=True)  9.33 us
    dot_general x16, matrix products, mul(): return jnp.einsum('mij,mjk->mik', a, b, precision=HIGH)  7.59 us
    all_to_all x1, waiting for transfers between devices, summed_gram(): lax.all_to_all(part, 'model', split_axis=0, concat_axis=0, tiled=True)  6.93 us
    dot_general x2, matrix products, summed_gram(): part = jnp.einsum('mik,mjk->mij', rows, rows, precision=HIGH)  4.93 us
  transfers between devices with their start and end apart: 1, of which 1 were waited for; matrix products, arithmetic and copies ran while one was open for 0% of the time, Pallas kernels for 0%

profile of v1, /device:TPU:1, one launch (start us, length us, event | category | flops | bytes accessed | tf_op | source)
XLA Modules:
  0.0 198.0 jit_solution(3235271127646908158)
XLA Ops:
  0.6 3.7 %multiply_add_fusion = f32[512,2,512]{2,1,0:T(2,128)S(1)} fusion(f32[512,2,512]{2,1,0:T(2,128)} %param.3, f32[512,2,512]{2,1,0:T(2,128)} %param.4), kind=kLoop, calls=%fused_computation.2 | loop fusion | flops 1048576 | bytes 6291456 | tf_op jit(solution)/shard_map/add | solution.py:34
  4.3 62.5 %all_to_all.46 = f32[512,2,512]{2,1,0:T(2,128)S(1)} all-to-all(f32[512,2,512]{2,1,0:T(2,128)S(1)} %multiply_add_fusion), channel_id=1, replica_groups=mesh['shard'=64,'model'=4] {'shard'}, dimensions={0} | all-to-all | bytes 4194304 | tf_op jit(solution)/shard_map/all_to_all | solution.py:35
  66.8 2.1 %copy.11 = f32[64,8,2,512]{3,2,0,1:T(2,128)} copy(f32[64,8,2,512]{3,2,1,0:T(2,128)S(1)} %bitcast.46) | data formatting | bytes 4194304 | tf_op jit(solution)/shard_map/all_to_all | solution.py:35
  68.9 2.7 %all_to_all.35 = f32[8,128,512]{2,1,0:T(8,128)S(1)} reshape(f32[8,64,2,512]{3,2,1,0:T(2,128)} %bitcast.44) | data formatting | bytes 4194304 | tf_op jit(solution)/shard_map/all_to_all | solution.py:35
  71.6 2.9 %fusion.8 = f32[8,128,128]{2,1,0:T(8,128)} fusion(f32[8,128,512]{2,1,0:T(8,128)S(1)} %all_to_all.35), kind=kOutput, calls=%fused_computation.22 | convolution fusion | flops 805306368 | bytes 2621440 | tf_op jit(solution)/shard_map/mik,mjk->mij/dot_general | solution.py:28
  74.4 4.2 %all-to-all-start.1 = ((f32[8,128,128]{2,1,0:T(8,128)}), f32[8,128,128]{2,1,0:T(8,128)S(1)}, u32[]{:S(2)}, u32[]{:S(2)}) async-start(f32[8,128,128]{2,1,0:T(8,128)} %fusion.8), calls=%async_computation.1 | async-start | bytes 1048576 | tf_op jit(solution)/shard_map/all_to_all | solution.py:29
  78.7 6.9 %all-to-all-done.1 = f32[8,128,128]{2,1,0:T(8,128)S(1)} async-done(((f32[8,128,128]{2,1,0:T(8,128)}), f32[8,128,128]{2,1,0:T(8,128)S(1)}, u32[]{:S(2)}, u32[]{:S(2)}) %all-to-all-start.1) | async-done | bytes 524320 | tf_op jit(solution)/shard_map/all_to_all | solution.py:29
  85.7 0.4 fusion.4
  86.1 0.3 fusion.5
  86.7 0.3 fusion.3
  87.0 0.3 convolution_multiply_fusion.3
  87.3 9.9 %all_gather.6 = f32[8,128,128]{2,1,0:T(8,128)S(1)} all-gather(f32[2,128,128]{2,1,0:T(8,128)S(1)} %convolution_multiply_fusion.3), channel_id=1, replica_groups=mesh['shard'=64,'model'=4] {'model'}, dimensions={0}, use_global_device_ids=true | all-gather | bytes 655360 | tf_op jit(solution)/shard_map/all_gather | solution.py:39
  97.2 1.9 fusion.10
  99.0 2.1 %fusion.11 = f32[8,128,128]{2,1,0:T(8,128)S(1)} fusion(f32[8,128,512]{2,1,0:T(8,128)S(1)} %fusion.10), kind=kOutput, calls=%fused_computation.25 | convolution fusion | flops 805306368 | bytes 2621440 | tf_op jit(solution)/shard_map/mik,mjk->mij/dot_general | solution.py:28
  101.1 9.3 %all_to_all.47 = f32[8,128,128]{2,1,0:T(8,128)S(1)} all-to-all(f32[8,128,128]{2,1,0:T(8,128)S(1)} %fusion.11), channel_id=1, replica_groups=mesh['shard'=64,'model'=4] {'model'}, dimensions={0} | all-to-all | bytes 1048576 | tf_op jit(solution)/shard_map/all_to_all | solution.py:29
  110.5 0.3 fusion.2
  111.3 0.3 fusion.1
  112.4 0.3 fusion
  113.0 10.5 %all_gather.7 = f32[8,128,128]{2,1,0:T(8,128)S(1)} all-gather(f32[2,128,128]{2,1,0:T(8,128)S(1)} %fusion.17), channel_id=1, replica_groups=mesh['shard'=64,'model'=4] {'model'}, dimensions={0}, use_global_device_ids=true | all-gather | bytes 655360 | tf_op jit(solution)/shard_map/all_gather | solution.py:41
  123.4 1.8 fusion.18
  125.3 1.2 copy.8
  126.5 66.2 %all_to_all.48 = f32[8,128,512]{2,0,1:T(8,128)S(1)} all-to-all(f32[8,128,512]{2,0,1:T(8,128)S(1)} %copy.8), channel_id=1, replica_groups=mesh['shard'=64,'model'=4] {'shard'}, dimensions={1} | all-to-all | bytes 4194304 | tf_op jit(solution)/shard_map/all_to_all | solution.py:42
  192.8 1.9 copy.9
  194.7 3.3 %bitcast_subtract_fusion = f32[512,2,512]{2,1,0:T(2,128)} fusion(f32[64,8,2,512]{3,2,1,0:T(2,128)S(1)} %copy.9, f32[512,2,512]{2,1,0:T(2,128)S(1)} %copy-done.3), kind=kLoop, calls=%fused_computation | loop fusion | flops 1048576 | bytes 6291456 | tf_op jit(solution)/shard_map/sub | solution.py:43
  (21 shorter events, 2.1 us)
Async XLA Ops:
  4.3 62.5 %copy-start.2 = (f32[512,2,512]{2,1,0:T(2,128)}, f32[512,2,512]{2,1,0:T(2,128)S(1)}, u32[]{:S(2)}) copy-start(f32[512,2,512]{2,1,0:T(2,128)S(1)} %multiply_add_fusion) | copy-start | bytes 6291460
  74.4 11.1 %all-to-all-start.1 = ((f32[8,128,128]{2,1,0:T(8,128)}), f32[8,128,128]{2,1,0:T(8,128)S(1)}, u32[]{:S(2)}, u32[]{:S(2)}) async-start(f32[8,128,128]{2,1,0:T(8,128)} %fusion.8), calls=%async_computation.1 | async-start | bytes 1048576 | tf_op jit(solution)/shard_map/all_to_all | solution.py:29
  99.0 2.1 %copy-start = (f32[8,128,512]{2,1,0:T(8,128)}, f32[8,128,512]{2,1,0:T(8,128)S(1)}, u32[]{:S(2)}) copy-start(f32[8,128,512]{2,1,0:T(8,128)S(1)} %fusion.10) | copy-start | bytes 6291460
  110.5 13.0 %copy-start.1 = (f32[8,128,512]{2,1,0:T(8,128)S(1)}, f32[8,128,512]{2,1,0:T(8,128)}, u32[]{:S(2)}) copy-start(f32[8,128,512]{2,1,0:T(8,128)} %copy-done) | copy-start | bytes 6291460
  192.8 1.9 copy-start.3

commit v2 on v1

v2 whole, which is shorter than its diff:
```python
import functools

import jax
import jax.numpy as jnp
from jax import lax
from jax.experimental import pallas as pl
from jax.experimental.pallas import tpu as pltpu
from jax.sharding import PartitionSpec as P

hold_rate = 0.95
learn_rate = 1.0
decay_rate = 0.1
HIGH = lax.Precision.HIGHEST
MESH = pl.DeviceIdType.MESH
F32 = jnp.float32

LANES = 128
TILE = 8
PAIR = 2
ROWS = PAIR * TILE


def mul(a, b):
    return lax.dot_general(a, b, (((1,), (0,)), ((), ())), precision=HIGH, preferred_element_type=F32)


def gram_of(x):
    return lax.dot_general(x, x, (((1,), (1,)), ((), ())), precision=HIGH, preferred_element_type=F32)


def diagonal(side):
    return lax.broadcasted_iota(jnp.int32, (side, side), 0) == lax.broadcasted_iota(jnp.int32, (side, side), 1)


def chain(grams, steps):
    eye = jnp.where(diagonal(grams[0].shape[0]), 3.4445, 0.0).astype(F32)
    totals = None
    for step in range(steps):
        squares = [mul(a, a) for a in grams]
        factors = [eye - 4.775 * a + 2.0315 * s for a, s in zip(grams, squares)]
        totals = factors if totals is None else [mul(f, t) for f, t in zip(factors, totals)]
        if step < steps - 1:
            half = [mul(f, a) for f, a in zip(factors, grams)]
            grams = [mul(h, f) for h, f in zip(half, factors)]
    return totals


def exchange_kernel(
    shards, models, chunks,
    grad, moment, back, held,
    grad_in, moment_in, rows, whole, moved, out, grams,
    in_sem, go_send, go_recv, gram_send, gram_recv, home_send, home_recv,
):
    me, mine = lax.axis_index("shard"), lax.axis_index("model")
    side = 2 * shards
    barrier = pltpu.get_barrier_semaphore()

    loads = [
        pltpu.make_async_copy(grad, grad_in, in_sem.at[0]),
        pltpu.make_async_copy(moment, moment_in, in_sem.at[1]),
    ]
    for load in loads:
        load.start()

    @pl.loop(1, shards)
    def _(step):
        pl.semaphore_signal(barrier, inc=1, device_id=(lax.rem(me + step, shards), mine), device_id_type=MESH)

    for step in range(1, models):
        pl.semaphore_signal(barrier, inc=1, device_id=(me, lax.rem(mine + step, models)), device_id_type=MESH)

    for load in loads:
        load.wait()

    @pl.loop(0, shards)
    def _(peer):
        held[peer] = hold_rate * moment_in[peer] + grad_in[peer]

    pl.semaphore_wait(barrier, shards - 1 + models - 1)

    def slot(peer):
        return pl.ds(pl.multiple_of(peer * ROWS, ROWS), ROWS)

    @pl.loop(0, chunks)
    def _(chunk):
        @pl.loop(1, shards)
        def _(step):
            peer = lax.rem(me + step, shards)
            pltpu.make_async_remote_copy(
                src_ref=held.at[peer, chunk], dst_ref=rows.at[chunk, slot(me)],
                send_sem=go_send, recv_sem=go_recv.at[chunk],
                device_id=(peer, mine), device_id_type=MESH,
            ).start()

        rows[chunk, slot(me)] = held[me, chunk]

    def landed(chunk):
        part = rows.at[chunk, pl.ds(0, (shards - 1) * ROWS)]
        return part

    def share_gram(turn, chunk):
        for step in range(1, models):
            peer = lax.rem(mine + step, models)
            pltpu.make_async_remote_copy(
                src_ref=grams.at[turn, chunk, mine], dst_ref=grams.at[turn, chunk, mine],
                send_sem=gram_send, recv_sem=gram_recv.at[turn, chunk],
                device_id=(me, peer), device_id_type=MESH,
            ).start()

    def summed_grams(turn, chunk):
        part = grams.at[turn, chunk, pl.ds(0, models - 1)]
        pltpu.make_async_copy(part, part, gram_recv.at[turn, chunk]).wait()
        sums = []
        for i in range(PAIR):
            total = grams[turn, chunk, 0, i]
            for k in range(1, models):
                total = total + grams[turn, chunk, k, i]
            sums.append(total)
        return sums

    def first_stage(chunk):
        part = landed(chunk)
        pltpu.make_async_copy(part, part, go_recv.at[chunk]).wait()
        for i in range(PAIR):
            for c in range(TILE // 2):
                for r in range(2):
                    whole[chunk, i, pl.ds(r * shards, shards), pl.ds(c * LANES, LANES)] = rows[
                        chunk, pl.ds(i * TILE + 2 * c + r, shards, stride=ROWS), :
                    ]
        for i in range(PAIR):
            grams[0, chunk, mine, i] = gram_of(whole[chunk, i])
        share_gram(0, chunk)

    def second_stage(chunk):
        sums = summed_grams(0, chunk)
        mask = diagonal(side)
        scales = [
            lax.rsqrt(jnp.sum(jnp.sum(jnp.where(mask, g, 0.0), axis=1, keepdims=True), axis=0, keepdims=True) + 1e-06)
            for g in sums
        ]
        factors = chain([g * s * s for g, s in zip(sums, scales)], 2)
        for i in range(PAIR):
            moved[chunk, i] = mul(factors[i] * scales[i], whole[chunk, i])
        for i in range(PAIR):
            grams[1, chunk, mine, i] = gram_of(moved[chunk, i])
        share_gram(1, chunk)

    def third_stage(chunk):
        factors = chain(summed_grams(1, chunk), 3)
        for i in range(PAIR):
            final = mul(factors[i], moved[chunk, i])
            for c in range(TILE // 2):
                for r in range(2):
                    out[chunk, pl.ds(i * TILE + 2 * c + r, shards, stride=ROWS), :] = final[
                        r * shards : (r + 1) * shards, c * LANES : (c + 1) * LANES
                    ]

        @pl.loop(1, shards)
        def _(step):
            peer = lax.rem(me + step, shards)
            pltpu.make_async_remote_copy(
                src_ref=out.at[chunk, slot(peer)], dst_ref=back.at[me, chunk],
                send_sem=home_send, recv_sem=home_recv,
                device_id=(peer, mine), device_id_type=MESH,
            ).start()

        back[me, chunk] = out[chunk, slot(me)]

    @pl.loop(0, chunks)
    def _(chunk):
        first_stage(chunk)

        @pl.when(chunk > 0)
        def _():
            third_stage(chunk - 1)

        second_stage(chunk)

    third_stage(chunks - 1)

    part = back.at[pl.ds(0, shards - 1)]
    pltpu.make_async_copy(part, part, home_recv).wait()
    pltpu.make_async_copy(part, part, home_send).wait()
    pltpu.make_async_copy(part, part, go_send).wait()
    part = grams.at[:, :, pl.ds(0, models - 1)]
    pltpu.make_async_copy(part, part, gram_send).wait()


def finish_kernel(back, held, weight, new_weights, new_momentum, result, sems):
    first = pltpu.make_async_copy(held, new_momentum, sems.at[0])
    first.start()

    @pl.loop(0, back.shape[0])
    def _(peer):
        result[peer] = (1.0 - learn_rate * decay_rate) * weight[peer] - learn_rate * back[peer]

    last = pltpu.make_async_copy(result, new_weights, sems.at[1])
    last.start()
    last.wait()
    first.wait()


def solution(mesh):
    shards, models = mesh.shape["shard"], mesh.shape["model"]

    def folded(x):
        mats, two, wide = x.shape
        x = x.reshape(mats, two, wide // LANES, LANES).transpose(0, 2, 1, 3)
        return x.reshape(shards, mats // (shards * PAIR), ROWS, LANES)

    def unfolded(x, like):
        mats, two, wide = like.shape
        x = x.reshape(mats, wide // LANES, two, LANES).transpose(0, 2, 1, 3)
        return x.reshape(like.shape)

    def on_device(grad_stack, moment_stack, weight_stack):
        grad, moment, weight = folded(grad_stack), folded(moment_stack), folded(weight_stack)
        shape = grad.shape
        chunks = shape[1]
        side, wide = 2 * shards, TILE // 2 * LANES
        vmem = pl.BlockSpec(memory_space=pltpu.VMEM)
        far = pl.BlockSpec(memory_space=pltpu.HBM)
        block = jax.ShapeDtypeStruct(shape, F32)
        back, held = pl.pallas_call(
            functools.partial(exchange_kernel, shards, models, chunks),
            name="exchange",
            out_shape=(block, block),
            in_specs=[far, far],
            out_specs=(vmem, vmem),
            scratch_shapes=[
                pltpu.VMEM(shape, F32),
                pltpu.VMEM(shape, F32),
                pltpu.VMEM((chunks, shards * ROWS, LANES), F32),
                pltpu.VMEM((chunks, PAIR, side, wide), F32),
                pltpu.VMEM((chunks, PAIR, side, wide), F32),
                pltpu.VMEM((chunks, shards * ROWS, LANES), F32),
                pltpu.VMEM((2, chunks, models, PAIR, side, side), F32),
                pltpu.SemaphoreType.DMA((2,)),
                pltpu.SemaphoreType.DMA,
                pltpu.SemaphoreType.DMA((chunks,)),
                pltpu.SemaphoreType.DMA,
                pltpu.SemaphoreType.DMA((2, chunks)),
                pltpu.SemaphoreType.DMA,
                pltpu.SemaphoreType.DMA,
            ],
            compiler_params=pltpu.CompilerParams(
                collective_id=0, has_side_effects=True, vmem_limit_bytes=40 * 1024 * 1024
            ),
        )(grad, moment)
        new_weights, new_momentum = pl.pallas_call(
            finish_kernel,
            name="finish",
            out_shape=(block, block),
            in_specs=[vmem, vmem, vmem],
            out_specs=(far, far),
            scratch_shapes=[pltpu.VMEM(shape, F32), pltpu.SemaphoreType.DMA((2,))],
            compiler_params=pltpu.CompilerParams(vmem_limit_bytes=16 * 1024 * 1024),
        )(back, held, weight)
        return unfolded(new_weights, weight_stack), unfolded(new_momentum, weight_stack)

    spec = P(None, "shard", "model")
    return jax.shard_map(on_device, mesh=mesh, in_specs=(spec,) * 3, out_specs=(spec,) * 2, check_vma=False)
```

time: 199 us -> 117 us (0.59)
  blocking collectives: 158 us -> 0 us
  Pallas kernels: 0 us -> 113 us
  matrix products: 12.5 us -> 0 us
  other arithmetic: 7.12 us -> 0 us
  waiting for transfers between devices: 6.93 us -> 0 us
  local copies, waits for them, and re-layouts: 7.95 us -> 3.18 us
  starting transfers between devices: 4.18 us -> 0 us
    all_to_all x3 -> x0, blocking collectives: 138 us -> none  [the longest x1 66.2 us: on_device(): lax.all_to_all(rows, 'shard', split_axis=1, concat_axis=0, tiled=True)]
    pallas_call x0 -> x2, Pallas kernels: none -> 113 us  [the longest x1 111 us: on_device(): pl.pallas_call(functools.partial(exchange_kernel, shards, models, chunks)...]
    all_gather x2 -> x0, blocking collectives: 20.4 us -> none  [the longest x1 10.5 us: on_device(): rows = mul(lax.all_gather(second, 'model', axis=0, tiled=True), rows)]
    dot_general x18 -> x0, matrix products: 12.5 us -> none  [the longest x16 7.59 us: mul(): return jnp.einsum('mij,mjk->mik', a, b, precision=HIGH)]
    all_to_all x1 -> x0, waiting for transfers between devices: 6.93 us -> none  [summed_gram(): lax.all_to_all(part, 'model', split_axis=0, concat_axis=0, tiled=True)]
    all_to_all x3 -> x0, local copies, waits for them, and re-layouts: 6.71 us -> none  [the longest x2 4.78 us: on_device(): lax.all_to_all(new_momentum, 'shard', split_axis=0, concat_axis=1, tiled=...]
    all_to_all x1 -> x0, starting transfers between devices: 4.18 us -> none  [summed_gram(): lax.all_to_all(part, 'model', split_axis=0, concat_axis=0, tiled=True)]
    add x1 -> x0, other arithmetic: 3.66 us -> none  [on_device(): new_momentum = hold_rate * moment_stack + grad_stack]
  transfers between devices with their start and end apart: 1 -> 0, of which waited for: 1 -> 0; matrix products, arithmetic and copies ran while one was open for 0% -> 0% of each run, Pallas kernels for 0% -> 0%
where the time goes in v2:
time: 117 us
  Pallas kernels  113 us (97%)
  local copies, waits for them, and re-layouts  3.18 us (3%)
    pallas_call x1, Pallas kernels, on_device(): pl.pallas_call(functools.partial(exchange_kernel, shards, models, chunks)...  111 us
    unnamed x6, local copies, waits for them, and re-layouts  3.18 us

profile of v2, /device:TPU:1, one launch (start us, length us, event | category | flops | bytes accessed | tf_op | source)
XLA Modules:
  0.0 116.8 jit_solution(13606344150115370626)
XLA Ops:
  0.6 0.0 copy-start.1
  0.6 1.6 %copy-done.1 = f32[512,2,512]{2,1,0:T(2,128)S(1)} copy-done((f32[512,2,512]{2,1,0:T(2,128)S(1)}, f32[512,2,512]{2,1,0:T(2,128)}, u32[]{:S(2)}) %copy-start.1) | copy-done | bytes 2097176
  2.2 0.0 copy-start.2
  2.2 1.6 %copy-done.2 = f32[512,2,512]{2,1,0:T(2,128)S(1)} copy-done((f32[512,2,512]{2,1,0:T(2,128)S(1)}, f32[512,2,512]{2,1,0:T(2,128)}, u32[]{:S(2)}) %copy-start.2) | copy-done | bytes 2097176
  3.8 0.0 copy-start
  3.8 110.9 %exchange.1 = (f32[64,4,16,128]{3,2,1,0:T(8,128)S(1)}, f32[64,4,16,128]{3,2,1,0:T(8,128)S(1)}) custom-call(f32[64,4,16,128]{3,2,1,0:T(8,128)S(1)} %bitcast.26, f32[64,4,16,128]{3,2,1,0:T(8,128)S(1)} %bitcast.27), custom_call_target="tpu_custom_call" | custom-call | tf_op jit(solution)/shard_map/exchange/pallas_call | solution.py:224
  114.8 0.0 copy-done
  114.8 2.0 %finish.1 = (f32[64,4,16,128]{3,2,1,0:T(8,128)}, f32[64,4,16,128]{3,2,1,0:T(8,128)}) custom-call(f32[64,4,16,128]{3,2,1,0:T(8,128)S(1)} %get-tuple-element.6.back, f32[64,4,16,128]{3,2,1,0:T(8,128)S(1)} %get-tuple-element.7.held, f32[64,4,16,128]{3,2,1,0:T(8,128)S(1)} %bitcast.25), custom_call_target="tpu_custom_call" | custom-call | tf_op jit(solution)/shard_map/finish/pallas_call | solution.py:250
Async XLA Ops:
  0.6 1.6 %copy-start.1 = (f32[512,2,512]{2,1,0:T(2,128)S(1)}, f32[512,2,512]{2,1,0:T(2,128)}, u32[]{:S(2)}) copy-start(f32[512,2,512]{2,1,0:T(2,128)} %param.3) | copy-start | bytes 6291460
  2.2 1.6 %copy-start.2 = (f32[512,2,512]{2,1,0:T(2,128)S(1)}, f32[512,2,512]{2,1,0:T(2,128)}, u32[]{:S(2)}) copy-start(f32[512,2,512]{2,1,0:T(2,128)} %param.4) | copy-start | bytes 6291460
  3.8 111.0 %copy-start = (f32[512,2,512]{2,1,0:T(2,128)S(1)}, f32[512,2,512]{2,1,0:T(2,128)}, u32[]{:S(2)}) copy-start(f32[512,2,512]{2,1,0:T(2,128)} %param.5) | copy-start | bytes 6291460

commit v3 on v2

--- a/solution.py
+++ b/solution.py
@@ -45,66 +45,73 @@
     return totals
 
 
+def peers_in_order(me, shards):
+    depth, flat = shards // 8, 8
+    z, rest = me // flat, lax.rem(me, flat)
+    x, core = rest // 2, lax.rem(rest, 2)
+    around = [0] + [d for k in range(1, depth) for d in (k, depth - k)][: depth - 1]
+    around = around[1:] + around[:1]
+    zs = [lax.rem(z + d, depth) * flat for d in around]
+    xs = [lax.rem(x + dx, 4) * 2 + lax.rem(core + dc, 2) for dx in (0, 1, 3, 2) for dc in (0, 1)]
+    order = [(zs[(i + j) % depth], xs[j], around[(i + j) % depth], j) for i in range(depth) for j in range(flat)]
+    return [a + b for a, b, d, j in order if (d, j) != (0, 0)]
+
+
 def exchange_kernel(
     shards, models, chunks,
-    grad, moment, back, held,
-    grad_in, moment_in, rows, whole, moved, out, grams,
+    grad, moment, weight, fresh, held,
+    grad_in, moment_in, weight_in, rows, whole, moved, out, back, grams,
     in_sem, go_send, go_recv, gram_send, gram_recv, home_send, home_recv,
 ):
     me, mine = lax.axis_index("shard"), lax.axis_index("model")
     side = 2 * shards
     barrier = pltpu.get_barrier_semaphore()
-
-    loads = [
-        pltpu.make_async_copy(grad, grad_in, in_sem.at[0]),
-        pltpu.make_async_copy(moment, moment_in, in_sem.at[1]),
-    ]
-    for load in loads:
-        load.start()
-
-    @pl.loop(1, shards)
-    def _(step):
-        pl.semaphore_signal(barrier, inc=1, device_id=(lax.rem(me + step, shards), mine), device_id_type=MESH)
-
-    for step in range(1, models):
-        pl.semaphore_signal(barrier, inc=1, device_id=(me, lax.rem(mine + step, models)), device_id_type=MESH)
-
-    for load in loads:
-        load.wait()
-
-    @pl.loop(0, shards)
-    def _(peer):
-        held[peer] = hold_rate * moment_in[peer] + grad_in[peer]
-
-    pl.semaphore_wait(barrier, shards - 1 + models - 1)
+    peers = peers_in_order(me, shards)
+    others = [lax.rem(mine + step, models) for step in range(1, models)]
+
+    for peer in peers:
+        pl.semaphore_signal(barrier, inc=1, device_id=(peer, mine), device_id_type=MESH)
+    for other in others:
+        pl.semaphore_signal(barrier, inc=1, device_id=(me, other), device_id_type=MESH)
+
+    def load(source, target, which, chunk):
+        return pltpu.make_async_copy(source.at[:, chunk], target.at[:, chunk], in_sem.at[which, chunk])
+
+    for chunk in range(chunks):
+        load(grad, grad_in, 0, chunk).start()
+        load(moment, moment_in, 1, chunk).start()
+    for chunk in range(chunks):
+        load(grad, grad_in, 0, chunk).wait()
+        load(moment, moment_in, 1, chunk).wait()
+        held[:, chunk] = hold_rate * moment_in[:, chunk] + grad_in[:, chunk]
+
+    pl.semaphore_wait(barrier, len(peers) + len(others))
 
     def slot(peer):
         return pl.ds(pl.multiple_of(peer * ROWS, ROWS), ROWS)
 
     @pl.loop(0, chunks)
     def _(chunk):
-        @pl.loop(1, shards)
-        def _(step):
-            peer = lax.rem(me + step, shards)
+        for peer in peers:
             pltpu.make_async_remote_copy(
                 src_ref=held.at[peer, chunk], dst_ref=rows.at[chunk, slot(me)],
                 send_sem=go_send, recv_sem=go_recv.at[chunk],
                 device_id=(peer, mine), device_id_type=MESH,
             ).start()
-
         rows[chunk, slot(me)] = held[me, chunk]
 
+    for chunk in range(chunks):
+        load(weight, weight_in, 2, chunk).start()
+
     def landed(chunk):
-        part = rows.at[chunk, pl.ds(0, (shards - 1) * ROWS)]
-        return part
+        return rows.at[chunk, pl.ds(0, (shards - 1) * ROWS)]
 
     def share_gram(turn, chunk):
-        for step in range(1, models):
-            peer = lax.rem(mine + step, models)
+        for other in others:
             pltpu.make_async_remote_copy(
                 src_ref=grams.at[turn, chunk, mine], dst_ref=grams.at[turn, chunk, mine],
                 send_sem=gram_send, recv_sem=gram_recv.at[turn, chunk],
-                device_id=(me, peer), device_id_type=MESH,
+                device_id=(me, other), device_id_type=MESH,
             ).start()
 
     def summed_grams(turn, chunk):
@@ -155,16 +162,13 @@
                         r * shards : (r + 1) * shards, c * LANES : (c + 1) * LANES
                     ]
 
-        @pl.loop(1, shards)
-        def _(step):
-            peer = lax.rem(me + step, shards)
+        for peer in peers:
             pltpu.make_async_remote_copy(
-                src_ref=out.at[chunk, slot(peer)], dst_ref=back.at[me, chunk],
-                send_sem=home_send, recv_sem=home_recv,
+                src_ref=out.at[chunk, slot(peer)], dst_ref=back.at[chunk, slot(me)],
+                send_sem=home_send, recv_sem=home_recv.at[chunk],
                 device_id=(peer, mine), device_id_type=MESH,
             ).start()
-
-        back[me, chunk] = out[chunk, slot(me)]
+        back[chunk, slot(me)] = out[chunk, slot(me)]
 
     @pl.loop(0, chunks)
     def _(chunk):
@@ -178,26 +182,33 @@
 
     third_stage(chunks - 1)
 
-    part = back.at[pl.ds(0, shards - 1)]
-    pltpu.make_async_copy(part, part, home_recv).wait()
+    for chunk in range(chunks):
+        load(weight, weight_in, 2, chunk).wait()
+        part = back.at[chunk, pl.ds(0, (shards - 1) * ROWS)]
+        pltpu.make_async_copy(part, part, home_recv.at[chunk]).wait()
+        fresh[:, chunk] = (1.0 - learn_rate * decay_rate) * weight_in[:, chunk] - learn_rate * back[chunk].reshape(
+            shards, ROWS, LANES
+        )
+
+    part = held.at[pl.ds(0, shards - 1)]
     pltpu.make_async_copy(part, part, home_send).wait()
     pltpu.make_async_copy(part, part, go_send).wait()
     part = grams.at[:, :, pl.ds(0, models - 1)]
     pltpu.make_async_copy(part, part, gram_send).wait()
 
 
-def finish_kernel(back, held, weight, new_weights, new_momentum, result, sems):
-    first = pltpu.make_async_copy(held, new_momentum, sems.at[0])
-    first.start()
-
-    @pl.loop(0, back.shape[0])
-    def _(peer):
-        result[peer] = (1.0 - learn_rate * decay_rate) * weight[peer] - learn_rate * back[peer]
-
-    last = pltpu.make_async_copy(result, new_weights, sems.at[1])
-    last.start()
-    last.wait()
-    first.wait()
+def write_kernel(fresh, held, new_weights, new_momentum, sems):
+    pieces = 4
+    size = fresh.shape[0] // pieces
+    copies = [
+        pltpu.make_async_copy(a.at[pl.ds(i * size, size)], b.at[pl.ds(i * size, size)], sems.at[k, i])
+        for k, (a, b) in enumerate(((held, new_momentum), (fresh, new_weights)))
+        for i in range(pieces)
+    ]
+    for copy in copies:
+        copy.start()
+    for copy in copies:
+        copy.wait()
 
 
 def solution(mesh):
@@ -221,41 +232,43 @@
         vmem = pl.BlockSpec(memory_space=pltpu.VMEM)
         far = pl.BlockSpec(memory_space=pltpu.HBM)
         block = jax.ShapeDtypeStruct(shape, F32)
-        back, held = pl.pallas_call(
+        fresh, held = pl.pallas_call(
             functools.partial(exchange_kernel, shards, models, chunks),
             name="exchange",
             out_shape=(block, block),
-            in_specs=[far, far],
+            in_specs=[far, far, far],
             out_specs=(vmem, vmem),
             scratch_shapes=[
+                pltpu.VMEM(shape, F32),
                 pltpu.VMEM(shape, F32),
                 pltpu.VMEM(shape, F32),
                 pltpu.VMEM((chunks, shards * ROWS, LANES), F32),
                 pltpu.VMEM((chunks, PAIR, side, wide), F32),
                 pltpu.VMEM((chunks, PAIR, side, wide), F32),
                 pltpu.VMEM((chunks, shards * ROWS, LANES), F32),
+                pltpu.VMEM((chunks, shards * ROWS, LANES), F32),
                 pltpu.VMEM((2, chunks, models, PAIR, side, side), F32),
-                pltpu.SemaphoreType.DMA((2,)),
+                pltpu.SemaphoreType.DMA((3, chunks)),
                 pltpu.SemaphoreType.DMA,
                 pltpu.SemaphoreType.DMA((chunks,)),
                 pltpu.SemaphoreType.DMA,
                 pltpu.SemaphoreType.DMA((2, chunks)),
                 pltpu.SemaphoreType.DMA,
-                pltpu.SemaphoreType.DMA,
+                pltpu.SemaphoreType.DMA((chunks,)),
             ],
             compiler_params=pltpu.CompilerParams(
-                collective_id=0, has_side_effects=True, vmem_limit_bytes=40 * 1024 * 1024
+                collective_id=0, has_side_effects=True, vmem_limit_bytes=48 * 1024 * 1024
             ),
-        )(grad, moment)
+        )(grad, moment, weight)
         new_weights, new_momentum = pl.pallas_call(
-            finish_kernel,
-            name="finish",
+            write_kernel,
+            name="write",
             out_shape=(block, block),
-            in_specs=[vmem, vmem, vmem],
+            in_specs=[vmem, vmem],
             out_specs=(far, far),
-            scratch_shapes=[pltpu.VMEM(shape, F32), pltpu.SemaphoreType.DMA((2,))],
+            scratch_shapes=[pltpu.SemaphoreType.DMA((2, 4))],
             compiler_params=pltpu.CompilerParams(vmem_limit_bytes=16 * 1024 * 1024),
-        )(back, held, weight)
+        )(fresh, held)
         return unfolded(new_weights, weight_stack), unfolded(new_momentum, weight_stack)
 
     spec = P(None, "shard", "model")

time: 117 us -> 113 us (0.966)
  local copies, waits for them, and re-layouts: 3.18 us -> 0 us
    unnamed x6 -> x0, local copies, waits for them, and re-layouts: 3.18 us -> none
where the time goes in v3:
time: 113 us
  Pallas kernels  112 us (99%)
    pallas_call x1, Pallas kernels, on_device(): pl.pallas_call(functools.partial(exchange_kernel, shards, models, chunks)...  110 us

profile of v3, /device:TPU:1, one launch (start us, length us, event | category | flops | bytes accessed | tf_op | source)
XLA Modules:
  0.0 112.8 jit_solution(6192625765474087890)
XLA Ops:
  0.6 110.0 %exchange.1 = (f32[64,4,16,128]{3,2,1,0:T(8,128)S(1)}, f32[64,4,16,128]{3,2,1,0:T(8,128)S(1)}) custom-call(f32[64,4,16,128]{3,2,1,0:T(8,128)} %bitcast.25, f32[64,4,16,128]{3,2,1,0:T(8,128)} %bitcast.26, f32[64,4,16,128]{3,2,1,0:T(8,128)} %bitcast.27), custom_call_target="tpu_custom_call" | custom-call | tf_op jit(solution)/shard_map/exchange/pallas_call | solution.py:235
  110.7 2.1 %write.1 = (f32[64,4,16,128]{3,2,1,0:T(8,128)}, f32[64,4,16,128]{3,2,1,0:T(8,128)}) custom-call(f32[64,4,16,128]{3,2,1,0:T(8,128)S(1)} %get-tuple-element.6.fresh, f32[64,4,16,128]{3,2,1,0:T(8,128)S(1)} %get-tuple-element.7.held), custom_call_target="tpu_custom_call" | custom-call | tf_op jit(solution)/shard_map/write/pallas_call | solution.py:263

commit v4 on v3

--- a/solution.py
+++ b/solution.py
@@ -16,7 +16,7 @@
 
 LANES = 128
 TILE = 8
-PAIR = 2
+PAIR = 1
 ROWS = PAIR * TILE
 
 
@@ -170,17 +170,19 @@
             ).start()
         back[chunk, slot(me)] = out[chunk, slot(me)]
 
-    @pl.loop(0, chunks)
-    def _(chunk):
-        first_stage(chunk)
-
-        @pl.when(chunk > 0)
+    @pl.loop(0, chunks + 2)
+    def _(turn):
+        @pl.when(turn < chunks)
         def _():
-            third_stage(chunk - 1)
-
-        second_stage(chunk)
-
-    third_stage(chunks - 1)
+            first_stage(turn)
+
+        @pl.when((turn >= 1) & (turn <= chunks))
+        def _():
+            second_stage(turn - 1)
+
+        @pl.when(turn >= 2)
+        def _():
+            third_stage(turn - 2)
 
     for chunk in range(chunks):
         load(weight, weight_in, 2, chunk).wait()

time: 113 us -> 107 us (0.947)
  Pallas kernels: 112 us -> 107 us
    pallas_call x1, Pallas kernels: 110 us -> 105 us  [on_device(): pl.pallas_call(functools.partial(exchange_kernel, shards, models, chunks)...]
where the time goes in v4:
time: 107 us
  Pallas kernels  107 us (100%)
    pallas_call x1, Pallas kernels, on_device(): pl.pallas_call(functools.partial(exchange_kernel, shards, models, chunks)...  105 us

profile of v4, /device:TPU:1, one launch (start us, length us, event | category | flops | bytes accessed | tf_op | source)
XLA Modules:
  0.0 107.2 jit_solution(13604192680245451358)
XLA Ops:
  0.6 104.5 %exchange.1 = (f32[64,8,8,128]{3,2,1,0:T(8,128)S(1)}, f32[64,8,8,128]{3,2,1,0:T(8,128)S(1)}) custom-call(f32[64,8,8,128]{3,2,1,0:T(8,128)} %bitcast.25, f32[64,8,8,128]{3,2,1,0:T(8,128)} %bitcast.26, f32[64,8,8,128]{3,2,1,0:T(8,128)} %bitcast.27), custom_call_target="tpu_custom_call" | custom-call | tf_op jit(solution)/shard_map/exchange/pallas_call | solution.py:237
  105.2 2.1 %write.1 = (f32[64,8,8,128]{3,2,1,0:T(8,128)}, f32[64,8,8,128]{3,2,1,0:T(8,128)}) custom-call(f32[64,8,8,128]{3,2,1,0:T(8,128)S(1)} %get-tuple-element.6.fresh, f32[64,8,8,128]{3,2,1,0:T(8,128)S(1)} %get-tuple-element.7.held), custom_call_target="tpu_custom_call" | custom-call | tf_op jit(solution)/shard_map/write/pallas_call | solution.py:265

commit v5 on v4

--- a/solution.py
+++ b/solution.py
@@ -45,32 +45,37 @@
     return totals
 
 
-def peers_in_order(me, shards):
-    depth, flat = shards // 8, 8
-    z, rest = me // flat, lax.rem(me, flat)
-    x, core = rest // 2, lax.rem(rest, 2)
-    around = [0] + [d for k in range(1, depth) for d in (k, depth - k)][: depth - 1]
-    around = around[1:] + around[:1]
-    zs = [lax.rem(z + d, depth) * flat for d in around]
-    xs = [lax.rem(x + dx, 4) * 2 + lax.rem(core + dc, 2) for dx in (0, 1, 3, 2) for dc in (0, 1)]
-    order = [(zs[(i + j) % depth], xs[j], around[(i + j) % depth], j) for i in range(depth) for j in range(flat)]
-    return [a + b for a, b, d, j in order if (d, j) != (0, 0)]
+def around(size):
+    return [d for k in range(1, size) for d in (k, size - k)][: size - 1]
 
 
 def exchange_kernel(
     shards, models, chunks,
     grad, moment, weight, fresh, held,
-    grad_in, moment_in, weight_in, rows, whole, moved, out, back, grams,
-    in_sem, go_send, go_recv, gram_send, gram_recv, home_send, home_recv,
+    grad_in, moment_in, weight_in, came, rows, whole, moved, out, left, back, grams,
+    in_sem, go_far_send, go_far_recv, go_near_send, go_near_recv, gram_send, gram_recv,
+    home_near_send, home_near_recv, home_far_send, home_far_recv,
 ):
     me, mine = lax.axis_index("shard"), lax.axis_index("model")
     side = 2 * shards
     barrier = pltpu.get_barrier_semaphore()
-    peers = peers_in_order(me, shards)
+    near_size = came.shape[1]
+    far_size = shards // near_size
+    far, near = me // near_size, lax.rem(me, near_size)
+    x, core = near // 2, lax.rem(near, 2)
+    fars = [lax.rem(far + d, far_size) for d in around(far_size)]
+    nears = [
+        lax.rem(x + dx, near_size // 2) * 2 + lax.rem(core + dc, 2)
+        for dx in [*around(near_size // 2), 0]
+        for dc in (0, 1)
+        if dx + dc > 0
+    ]
     others = [lax.rem(mine + step, models) for step in range(1, models)]
 
-    for peer in peers:
-        pl.semaphore_signal(barrier, inc=1, device_id=(peer, mine), device_id_type=MESH)
+    for peer in fars:
+        pl.semaphore_signal(barrier, inc=1, device_id=(peer * near_size + near, mine), device_id_type=MESH)
+    for peer in nears:
+        pl.semaphore_signal(barrier, inc=1, device_id=(far * near_size + peer, mine), device_id_type=MESH)
     for other in others:
         pl.semaphore_signal(barrier, inc=1, device_id=(me, other), device_id_type=MESH)
 
@@ -80,31 +85,54 @@
     for chunk in range(chunks):
         load(grad, grad_in, 0, chunk).start()
         load(moment, moment_in, 1, chunk).start()
-    for chunk in range(chunks):
+
+    def ready(chunk):
         load(grad, grad_in, 0, chunk).wait()
         load(moment, moment_in, 1, chunk).wait()
         held[:, chunk] = hold_rate * moment_in[:, chunk] + grad_in[:, chunk]
 
-    pl.semaphore_wait(barrier, len(peers) + len(others))
+    ready(0)
+    pl.semaphore_wait(barrier, len(fars) + len(nears) + len(others))
+
+    def group(peer):
+        size = far_size * ROWS
+        return pl.ds(pl.multiple_of(peer * size, size), size)
 
     def slot(peer):
         return pl.ds(pl.multiple_of(peer * ROWS, ROWS), ROWS)
 
+    def targets(peer):
+        return pl.ds(pl.multiple_of(peer * near_size, near_size), near_size)
+
+    def landed(ref, sem):
+        pltpu.make_async_copy(ref, ref, sem).wait()
+
+    for chunk in range(chunks):
+        for peer in fars:
+            pltpu.make_async_remote_copy(
+                src_ref=held.at[targets(peer), chunk], dst_ref=came.at[chunk, :, slot(far)],
+                send_sem=go_far_send, recv_sem=go_far_recv.at[chunk],
+                device_id=(peer * near_size + near, mine), device_id_type=MESH,
+            ).start()
+        if chunk + 1 < chunks:
+            ready(chunk + 1)
+
     @pl.loop(0, chunks)
     def _(chunk):
-        for peer in peers:
-            pltpu.make_async_remote_copy(
-                src_ref=held.at[peer, chunk], dst_ref=rows.at[chunk, slot(me)],
-                send_sem=go_send, recv_sem=go_recv.at[chunk],
-                device_id=(peer, mine), device_id_type=MESH,
-            ).start()
-        rows[chunk, slot(me)] = held[me, chunk]
+        came[chunk, :, slot(far)] = held[targets(far), chunk]
 
     for chunk in range(chunks):
         load(weight, weight_in, 2, chunk).start()
 
-    def landed(chunk):
-        return rows.at[chunk, pl.ds(0, (shards - 1) * ROWS)]
+    def relay_out(chunk):
+        landed(came.at[chunk, :, pl.ds(0, (far_size - 1) * ROWS)], go_far_recv.at[chunk])
+        for peer in nears:
+            pltpu.make_async_remote_copy(
+                src_ref=came.at[chunk, peer], dst_ref=rows.at[chunk, group(near)],
+                send_sem=go_near_send, recv_sem=go_near_recv.at[chunk],
+                device_id=(far * near_size + peer, mine), device_id_type=MESH,
+            ).start()
+        rows[chunk, group(near)] = came[chunk, near]
 
     def share_gram(turn, chunk):
         for other in others:
@@ -115,8 +143,7 @@
             ).start()
 
     def summed_grams(turn, chunk):
-        part = grams.at[turn, chunk, pl.ds(0, models - 1)]
-        pltpu.make_async_copy(part, part, gram_recv.at[turn, chunk]).wait()
+        landed(grams.at[turn, chunk, pl.ds(0, models - 1)], gram_recv.at[turn, chunk])
         sums = []
         for i in range(PAIR):
             total = grams[turn, chunk, 0, i]
@@ -126,8 +153,7 @@
         return sums
 
     def first_stage(chunk):
-        part = landed(chunk)
-        pltpu.make_async_copy(part, part, go_recv.at[chunk]).wait()
+        landed(rows.at[chunk, pl.ds(0, (near_size - 1) * far_size * ROWS)], go_near_recv.at[chunk])
         for i in range(PAIR):
             for c in range(TILE // 2):
                 for r in range(2):
@@ -162,41 +188,47 @@
                         r * shards : (r + 1) * shards, c * LANES : (c + 1) * LANES
                     ]
 
-        for peer in peers:
-            pltpu.make_async_remote_copy(
-                src_ref=out.at[chunk, slot(peer)], dst_ref=back.at[chunk, slot(me)],
-                send_sem=home_send, recv_sem=home_recv.at[chunk],
-                device_id=(peer, mine), device_id_type=MESH,
-            ).start()
-        back[chunk, slot(me)] = out[chunk, slot(me)]
-
-    @pl.loop(0, chunks + 2)
+        left[chunk, near] = out[chunk, group(near)]
+        for peer in nears:
+            pltpu.make_async_remote_copy(
+                src_ref=out.at[chunk, group(peer)], dst_ref=left.at[chunk, near],
+                send_sem=home_near_send, recv_sem=home_near_recv.at[chunk],
+                device_id=(far * near_size + peer, mine), device_id_type=MESH,
+            ).start()
+
+    def relay_home(chunk):
+        landed(left.at[chunk, pl.ds(0, near_size - 1)], home_near_recv.at[chunk])
+        for peer in fars:
+            pltpu.make_async_remote_copy(
+                src_ref=left.at[chunk, :, slot(peer)], dst_ref=back.at[chunk, far],
+                send_sem=home_far_send, recv_sem=home_far_recv.at[chunk],
+                device_id=(peer * near_size + near, mine), device_id_type=MESH,
+            ).start()
+        back[chunk, far] = left[chunk, :, slot(far)]
+
+    stages = (relay_out, first_stage, second_stage, third_stage, relay_home)
+    delays = (0, 1, 2, 3, 4)
+
+    @pl.loop(0, chunks + delays[-1])
     def _(turn):
-        @pl.when(turn < chunks)
-        def _():
-            first_stage(turn)
-
-        @pl.when((turn >= 1) & (turn <= chunks))
-        def _():
-            second_stage(turn - 1)
-
-        @pl.when(turn >= 2)
-        def _():
-            third_stage(turn - 2)
+        for late, stage in zip(delays, stages):
+
+            @pl.when((turn >= late) & (turn < chunks + late))
+            def _():
+                stage(turn - late)
 
     for chunk in range(chunks):
         load(weight, weight_in, 2, chunk).wait()
-        part = back.at[chunk, pl.ds(0, (shards - 1) * ROWS)]
-        pltpu.make_async_copy(part, part, home_recv.at[chunk]).wait()
+        landed(back.at[chunk, pl.ds(0, far_size - 1)], home_far_recv.at[chunk])
         fresh[:, chunk] = (1.0 - learn_rate * decay_rate) * weight_in[:, chunk] - learn_rate * back[chunk].reshape(
             shards, ROWS, LANES
         )
 
-    part = held.at[pl.ds(0, shards - 1)]
-    pltpu.make_async_copy(part, part, home_send).wait()
-    pltpu.make_async_copy(part, part, go_send).wait()
-    part = grams.at[:, :, pl.ds(0, models - 1)]
-    pltpu.make_async_copy(part, part, gram_send).wait()
+    for sem in (go_far_send, home_far_send):
+        landed(came.at[:, :, pl.ds(0, (far_size - 1) * ROWS)], sem)
+    for sem in (go_near_send, home_near_send):
+        landed(came.at[:, pl.ds(0, near_size - 1)], sem)
+    landed(grams.at[:, :, pl.ds(0, models - 1)], gram_send)
 
 
 def write_kernel(fresh, held, new_weights, new_momentum, sems):
@@ -231,30 +263,37 @@
         shape = grad.shape
         chunks = shape[1]
         side, wide = 2 * shards, TILE // 2 * LANES
+        near, far = 8, shards // 8
         vmem = pl.BlockSpec(memory_space=pltpu.VMEM)
-        far = pl.BlockSpec(memory_space=pltpu.HBM)
+        hbm = pl.BlockSpec(memory_space=pltpu.HBM)
         block = jax.ShapeDtypeStruct(shape, F32)
         fresh, held = pl.pallas_call(
             functools.partial(exchange_kernel, shards, models, chunks),
             name="exchange",
             out_shape=(block, block),
-            in_specs=[far, far, far],
+            in_specs=[hbm, hbm, hbm],
             out_specs=(vmem, vmem),
             scratch_shapes=[
                 pltpu.VMEM(shape, F32),
                 pltpu.VMEM(shape, F32),
                 pltpu.VMEM(shape, F32),
+                pltpu.VMEM((chunks, near, far * ROWS, LANES), F32),
                 pltpu.VMEM((chunks, shards * ROWS, LANES), F32),
                 pltpu.VMEM((chunks, PAIR, side, wide), F32),
                 pltpu.VMEM((chunks, PAIR, side, wide), F32),
                 pltpu.VMEM((chunks, shards * ROWS, LANES), F32),
-                pltpu.VMEM((chunks, shards * ROWS, LANES), F32),
+                pltpu.VMEM((chunks, near, far * ROWS, LANES), F32),
+                pltpu.VMEM((chunks, far, near, ROWS, LANES), F32),
                 pltpu.VMEM((2, chunks, models, PAIR, side, side), F32),
                 pltpu.SemaphoreType.DMA((3, chunks)),
                 pltpu.SemaphoreType.DMA,
                 pltpu.SemaphoreType.DMA((chunks,)),
                 pltpu.SemaphoreType.DMA,
+                pltpu.SemaphoreType.DMA((chunks,)),
+                pltpu.SemaphoreType.DMA,
                 pltpu.SemaphoreType.DMA((2, chunks)),
+                pltpu.SemaphoreType.DMA,
+                pltpu.SemaphoreType.DMA((chunks,)),
                 pltpu.SemaphoreType.DMA,
                 pltpu.SemaphoreType.DMA((chunks,)),
             ],
@@ -267,7 +306,7 @@
             name="write",
             out_shape=(block, block),
             in_specs=[vmem, vmem],
-            out_specs=(far, far),
+            out_specs=(hbm, hbm),
             scratch_shapes=[pltpu.SemaphoreType.DMA((2, 4))],
             compiler_params=pltpu.CompilerParams(vmem_limit_bytes=16 * 1024 * 1024),
         )(fresh, held)

time: 107 us -> 105 us (0.981)
  Pallas kernels: 107 us -> 105 us
    pallas_call x1, Pallas kernels: 105 us -> 103 us  [on_device(): pl.pallas_call(functools.partial(exchange_kernel, shards, models, chunks)...]
where the time goes in v5:
time: 105 us
  Pallas kernels  105 us (100%)
    pallas_call x1, Pallas kernels, on_device(): pl.pallas_call(functools.partial(exchange_kernel, shards, models, chunks)...  103 us

profile of v5, /device:TPU:1, one launch (start us, length us, event | category | flops | bytes accessed | tf_op | source)
XLA Modules:
  0.0 105.4 jit_solution(13920832063067929859)
XLA Ops:
  0.6 102.7 %exchange.1 = (f32[64,8,8,128]{3,2,1,0:T(8,128)S(1)}, f32[64,8,8,128]{3,2,1,0:T(8,128)S(1)}) custom-call(f32[64,8,8,128]{3,2,1,0:T(8,128)} %bitcast.25, f32[64,8,8,128]{3,2,1,0:T(8,128)} %bitcast.26, f32[64,8,8,128]{3,2,1,0:T(8,128)} %bitcast.27), custom_call_target="tpu_custom_call" | custom-call | tf_op jit(solution)/shard_map/exchange/pallas_call | solution.py:270
  103.3 2.1 %write.1 = (f32[64,8,8,128]{3,2,1,0:T(8,128)}, f32[64,8,8,128]{3,2,1,0:T(8,128)}) custom-call(f32[64,8,8,128]{3,2,1,0:T(8,128)S(1)} %get-tuple-element.6.fresh, f32[64,8,8,128]{3,2,1,0:T(8,128)S(1)} %get-tuple-element.7.held), custom_call_target="tpu_custom_call" | custom-call | tf_op jit(solution)/shard_map/write/pallas_call | solution.py:304

commit v6 on v5

--- a/solution.py
+++ b/solution.py
@@ -198,7 +198,7 @@
 
     def relay_home(chunk):
         landed(left.at[chunk, pl.ds(0, near_size - 1)], home_near_recv.at[chunk])
-        for peer in fars:
+        for peer in reversed(fars):
             pltpu.make_async_remote_copy(
                 src_ref=left.at[chunk, :, slot(peer)], dst_ref=back.at[chunk, far],
                 send_sem=home_far_send, recv_sem=home_far_recv.at[chunk],

time: 105 us -> 104 us (level)
  Pallas kernels: 105 us -> 103 us
    pallas_call x1, Pallas kernels: 103 us -> 101 us  [on_device(): pl.pallas_call(functools.partial(exchange_kernel, shards, models, chunks)...]
where the time goes in v6:
time: 104 us
  Pallas kernels  103 us (99%)
    pallas_call x1, Pallas kernels, on_device(): pl.pallas_call(functools.partial(exchange_kernel, shards, models, chunks)...  101 us

profile of v6, /device:TPU:1, one launch (start us, length us, event | category | flops | bytes accessed | tf_op | source)
XLA Modules:
  0.0 103.7 jit_solution(8495382040239089200)
XLA Ops:
  0.6 101.0 %exchange.1 = (f32[64,8,8,128]{3,2,1,0:T(8,128)S(1)}, f32[64,8,8,128]{3,2,1,0:T(8,128)S(1)}) custom-call(f32[64,8,8,128]{3,2,1,0:T(8,128)} %bitcast.25, f32[64,8,8,128]{3,2,1,0:T(8,128)} %bitcast.26, f32[64,8,8,128]{3,2,1,0:T(8,128)} %bitcast.27), custom_call_target="tpu_custom_call" | custom-call | tf_op jit(solution)/shard_map/exchange/pallas_call | solution.py:270
  101.6 2.1 %write.1 = (f32[64,8,8,128]{3,2,1,0:T(8,128)}, f32[64,8,8,128]{3,2,1,0:T(8,128)}) custom-call(f32[64,8,8,128]{3,2,1,0:T(8,128)S(1)} %get-tuple-element.6.fresh, f32[64,8,8,128]{3,2,1,0:T(8,128)S(1)} %get-tuple-element.7.held), custom_call_target="tpu_custom_call" | custom-call | tf_op jit(solution)/shard_map/write/pallas_call | solution.py:304

commit v7 on v6

--- a/solution.py
+++ b/solution.py
@@ -66,7 +66,7 @@
     fars = [lax.rem(far + d, far_size) for d in around(far_size)]
     nears = [
         lax.rem(x + dx, near_size // 2) * 2 + lax.rem(core + dc, 2)
-        for dx in [*around(near_size // 2), 0]
+        for dx in [*reversed(around(near_size // 2)), 0]
         for dc in (0, 1)
         if dx + dc > 0
     ]

time: 104 us -> 104 us (level)
  no operation moved by 1% of the time
where the time goes in v7:
time: 104 us; the launch traced here: 103 us
  Pallas kernels  102 us (98%)
    pallas_call x1, Pallas kernels, on_device(): pl.pallas_call(functools.partial(exchange_kernel, shards, models, chunks)...  100 us

profile of v7, /device:TPU:1, one launch (start us, length us, event | category | flops | bytes accessed | tf_op | source)
XLA Modules:
  0.0 103.0 jit_solution(10160965209161599870)
XLA Ops:
  0.6 100.3 %exchange.1 = (f32[64,8,8,128]{3,2,1,0:T(8,128)S(1)}, f32[64,8,8,128]{3,2,1,0:T(8,128)S(1)}) custom-call(f32[64,8,8,128]{3,2,1,0:T(8,128)} %bitcast.25, f32[64,8,8,128]{3,2,1,0:T(8,128)} %bitcast.26, f32[64,8,8,128]{3,2,1,0:T(8,128)} %bitcast.27), custom_call_target="tpu_custom_call" | custom-call | tf_op jit(solution)/shard_map/exchange/pallas_call | solution.py:270
  100.9 2.1 %write.1 = (f32[64,8,8,128]{3,2,1,0:T(8,128)}, f32[64,8,8,128]{3,2,1,0:T(8,128)}) custom-call(f32[64,8,8,128]{3,2,1,0:T(8,128)S(1)} %get-tuple-element.6.fresh, f32[64,8,8,128]{3,2,1,0:T(8,128)S(1)} %get-tuple-element.7.held), custom_call_target="tpu_custom_call" | custom-call | tf_op jit(solution)/shard_map/write/pallas_call | solution.py:304
